TPU v7x, 16 devices: a whole 2x2x2 slice. The times are simulated.
16 devices in a mesh: dp: 4 (over z, y), seq: 4 (over x, core).
Axes of the slice: x: 2, y: 2, z: 2, core: 2. Of those that a mesh axis runs over, the one named last changes fastest.
Arguments:
- enc_out: bfloat16 [256, 8, 640], P('dp', 'seq'), parts along dimension 0
- pred_out: bfloat16 [256, 32, 640], P('dp'), parts along dimension 0
- w_enc: bfloat16 [640, 640], replicated
- w_pred: bfloat16 [640, 640], replicated
- w_out: bfloat16 [640, 1024], replicated
- labels: int32 [256, 31], P('dp'), parts along dimension 0
- frame_len: int32 [256], P('dp'), parts along dimension 0
- label_len: int32 [256], P('dp'), parts along dimension 0
Outputs:
- output 1: float32 [256], P('dp'), parts along dimension 0
- output 2: bfloat16 [256, 8, 640], P('dp', 'seq'), parts along dimension 0
- output 3: float32 [2560, 640], P('dp'), parts along dimension 0
- output 4: float32 [2560, 640], P('dp'), parts along dimension 0
- output 5: float32 [2560, 1024], P('dp'), parts along dimension 0
There are 4 independent parts. A program takes and returns all parts, laid end to end along the dimension named above; an argument that names none is the same for every part.
All inputs are finite; a program needn't handle non-finite values.
Results may differ from a plain program's by a relative error of at most 0.0138912.
Values are sent between devices in bfloat16 or wider.
A program may use at most 1 GiB of HBM per device.

v0:
```python
import functools

import jax
import jax.numpy as jnp
from jax import lax
from jax.experimental import pallas as pl
from jax.experimental.pallas import tpu as pltpu
from jax.sharding import PartitionSpec as P

NEG = -1.0e30
ROWS = 256
WIN = 6
CHUNK = 256
CORE_MIN, CORE_MAX = 24, 40
GATHER_VMEM = 40 << 20
CORE_VMEM = 47 << 20
REDUCE_VMEM = 36 << 20
STORE_VMEM = 1 << 20
KEEP = 15
F32 = jnp.float32
BF16 = jnp.bfloat16
MESH = pl.DeviceIdType.MESH
NT = (((1,), (1,)), ((), ()))
NN = (((1,), (0,)), ((), ()))


def dot(a, b, dims=NN):
    return lax.dot_general(a, b, dims, preferred_element_type=F32)


def in_hbm(x):
    return pltpu.with_memory_space_constraint(x, pltpu.HBM)


def in_vmem(x):
    return pltpu.with_memory_space_constraint(x, pltpu.VMEM)


def split3(x):
    hi = x.astype(BF16).astype(F32)
    r1 = x - hi
    mid = r1.astype(BF16).astype(F32)
    return hi, mid, r1 - mid


def logadd(a, b):
    m = jnp.maximum(a, b)
    return m + jnp.log(1.0 + jnp.exp(jnp.minimum(a, b) - m))


def label_rows(n_u, first, n_rows, lab_ref):
    lab = lab_ref[...]
    n_lab, n_utt = lab.shape
    pad = jnp.zeros((n_u - n_lab, n_utt), F32)
    parts = [lax.shift_right_arithmetic(lab, 5).astype(F32), pad, jnp.bitwise_and(lab, 31).astype(F32), pad]
    both = jnp.concatenate(parts, axis=0).T.astype(BF16)
    row = lax.broadcasted_iota(jnp.int32, (n_rows, n_utt), 0)
    col = lax.broadcasted_iota(jnp.int32, (n_rows, n_utt), 1)
    spread = dot(jnp.where(row // n_u + first == col, 1.0, 0.0).astype(BF16), both)
    row = lax.broadcasted_iota(jnp.int32, (n_rows, 2 * n_u), 0)
    col = lax.broadcasted_iota(jnp.int32, (n_rows, 2 * n_u), 1)
    own = jnp.where(row % n_u == col % n_u, spread, 0.0).astype(BF16)
    place = (lax.broadcasted_iota(jnp.int32, (2 * n_u, 128), 0) // n_u == lax.broadcasted_iota(jnp.int32, (2 * n_u, 128), 1))
    return dot(own, jnp.where(place, 1.0, 0.0).astype(BF16)).astype(BF16)


def gather_kernel(n_t, n_u, enc_h, g_h, we_h, wp_h, wo_h, lab_h, c_ref, a_ref, wot_ref, f_ref, y_ref,
                  enc_ref, g_ref, we_ref, wp_ref, wo_ref, lab_ref, fbuf, in_sem, send_sem, recv_sem):
    me = lax.axis_index('seq')
    n_seq = fbuf.shape[0]
    partner = me + 1 - 2 * (me % 2)
    peer = (me + 2) % n_seq
    load_enc, load_wo, load_wp, load_g, load_we, load_lab = loads = [pltpu.make_async_copy(src, dst, in_sem.at[q]) for q, (src, dst) in enumerate(
        ((enc_h, enc_ref), (wo_h, wo_ref), (wp_h, wp_ref), (g_h, g_ref), (we_h, we_ref), (lab_h, lab_ref)))]
    for load in loads:
        load.start()
    barrier = pltpu.get_barrier_semaphore()
    for other in (partner, peer):
        pl.semaphore_signal(barrier, inc=1, device_id={'seq': other}, device_id_type=MESH)
    pl.semaphore_wait(barrier, 2)

    def send(src, slot, sem, other):
        return pltpu.make_async_remote_copy(src_ref=src, dst_ref=fbuf.at[slot], send_sem=send_sem.at[sem], recv_sem=recv_sem.at[sem],
                                            device_id={'seq': other}, device_id_type=MESH)
    load_enc.wait()
    to_peer = send(enc_ref, me, 0, peer)
    to_peer.start()
    to_partner = send(enc_ref, me, 1, partner)
    to_partner.start()
    fbuf[me] = enc_ref[...]
    load_wo.wait()
    wot_ref[...] = wo_ref[...].T
    load_wp.wait()
    load_g.wait()
    n_own_utt = CORE_MAX + WIN
    n_c = n_own_utt * n_u
    first = me % 2 * (c_ref.shape[0] // n_u - n_own_utt)
    rows_c = pl.ds(pl.multiple_of(first * n_u, 64), n_c)
    c_ref[rows_c, :] = dot(g_ref[rows_c, :], wp_ref[...]).astype(BF16)
    load_we.wait()
    load_lab.wait()
    y_ref[rows_c, :] = label_rows(n_u, first, n_c, lab_ref)
    n_f, n_h = f_ref.shape
    n_own = n_f // n_seq
    n_loc = n_t // n_seq
    col = lax.broadcasted_iota(jnp.int32, (n_f, n_own), 0)
    row = lax.broadcasted_iota(jnp.int32, (n_f, n_own), 1)

    def piece(p):
        rows = fbuf[p].reshape(n_own, n_h)
        f_ref[pl.ds(pl.multiple_of(p * n_own, n_own), n_own), :] = rows
        order = jnp.where(col == row // n_loc * n_t + p * n_loc + row % n_loc, 1.0, 0.0).astype(BF16)
        return dot(order, dot(rows, we_ref[...]).astype(BF16))
    a_t = piece(me)
    to_partner.wait_recv()
    a_t = a_t + piece(partner)
    to_peer.wait_recv()
    relay = send(fbuf.at[peer], peer, 2, partner)
    relay.start()
    a_t = a_t + piece(peer)
    relay.wait_recv()
    a_ref[...] = a_t + piece((partner + 2) % n_seq)
    to_peer.wait_send()
    to_partner.wait_send()
    relay.wait_send()


def gather_call(enc, g2, w_enc, w_pred, w_out, labels_t, n_seq, n_t, n_u):
    n_utt, n_loc, n_h = enc.shape
    n_j = w_enc.shape[1]
    vm = pl.BlockSpec(memory_space=pltpu.VMEM)
    n_f = n_utt * n_loc * n_seq
    args = [in_hbm(x) for x in (enc, g2, w_enc, w_pred, w_out, labels_t)]
    return pl.pallas_call(
        functools.partial(gather_kernel, n_t, n_u),
        out_shape=(
            pltpu.VMEM((g2.shape[0], n_j), BF16),
            pltpu.VMEM((n_f, n_j), F32),
            pltpu.VMEM(w_out.shape[::-1], BF16),
            pltpu.VMEM((n_f, n_h), BF16),
            pltpu.VMEM((g2.shape[0], 128), BF16),
        ),
        in_specs=[pl.BlockSpec(memory_space=pltpu.HBM)] * 6,
        out_specs=(vm,) * 5,
        scratch_shapes=[pltpu.VMEM(x.shape, x.dtype) for x in (enc, g2, w_enc, w_pred, w_out, labels_t)] + [
            pltpu.VMEM((n_seq, n_utt, n_loc, n_h), BF16),
            pltpu.SemaphoreType.DMA((6,)),
            pltpu.SemaphoreType.DMA((3,)),
            pltpu.SemaphoreType.DMA((3,)),
        ],
        compiler_params=pltpu.CompilerParams(collective_id=0, has_side_effects=True, vmem_limit_bytes=GATHER_VMEM),
        name="rnnt_gather",
    )(*args)


def reduce_kernel(n_t, gwo_v, dc_v, da_v, loss_v, f_v, g_p, we_p, loss_ref, gf_ref, gwe_ref, gwp_ref, gwo_ref,
                  g_v, we_v, gwp_v, rgwo, rgwp, rda, rloss, da_rows, in_sem, send_sem, recv_sem):
    me = lax.axis_index('seq')
    partner = me + 1 - 2 * (me % 2)
    loads = [pltpu.make_async_copy(src, dst, in_sem.at[q]) for q, (src, dst) in enumerate(((g_p, g_v), (we_p, we_v)))]
    for load in loads:
        load.start()
    barrier = pltpu.get_barrier_semaphore()
    pl.semaphore_signal(barrier, inc=1, device_id={'seq': partner}, device_id_type=MESH)
    pl.semaphore_wait(barrier, 1)

    def send(src, dst, sem):
        return pltpu.make_async_remote_copy(src_ref=src, dst_ref=dst, send_sem=send_sem.at[sem], recv_sem=recv_sem.at[sem],
                                            device_id={'seq': partner}, device_id_type=MESH)
    n_part = 4
    rows = gwo_v.shape[0] // n_part
    n_da = CORE_MAX * n_t
    da_lo = (da_v.shape[0] - n_da) * (me % 2)
    part = pl.ds(pl.multiple_of(da_lo, 64), n_da)
    sends = [send(da_v.at[part], rda.at[part], 0), send(loss_v, rloss, 1)]
    sends += [send(gwo_v.at[pl.ds(q * rows, rows)], rgwo.at[pl.ds(q * rows, rows)], 2 + q) for q in range(n_part)]
    for s in sends:
        s.start()
    loads[0].wait()
    gwp_v[...] = dot(g_v[...].T, dc_v[...].astype(BF16))
    s_gwp = send(gwp_v, rgwp, 2 + n_part)
    loads[1].wait()
    sends[0].wait_recv()
    sends[1].wait_recv()
    loss_ref[...] = (loss_v[0:1, :] + rloss[0:1, :])[:, 0:loss_ref.shape[1]]
    row = lax.broadcasted_iota(jnp.int32, rda.shape, 0) - (da_v.shape[0] - n_da) * (partner % 2)
    other = jnp.where((row >= 0) & (row < n_da), rda[...].astype(F32), 0.0)
    da = (da_v[...].astype(F32) + other).astype(BF16)
    s_gwp.start()
    n_f = da.shape[0]
    n_loc = gf_ref.shape[1]
    n_own = gf_ref.shape[0] * n_loc
    row = lax.broadcasted_iota(jnp.int32, (n_f, n_f), 0)
    col = lax.broadcasted_iota(jnp.int32, (n_f, n_f), 1)
    order = jnp.where(col == row % n_own // n_loc * n_t + row // n_own * n_loc + row % n_loc, 1.0, 0.0).astype(BF16)
    da_f = dot(order, da).astype(BF16)
    da_rows[...] = da_f
    gwe_ref[...] = dot(f_v[...].T, da_f)
    own = da_rows[pl.ds(pl.multiple_of(me * n_own, n_own), n_own), :]
    gf_ref[...] = dot(own, we_v[...], NT).astype(BF16).reshape(gf_ref.shape)
    for q in range(n_part):
        sends[2 + q].wait_recv()
        part = slice(q * rows, (q + 1) * rows)
        gwo_ref[part] = gwo_v[part] + rgwo[part]
    s_gwp.wait_recv()
    gwp_ref[...] = gwp_v[...] + rgwp[...]
    for s in sends + [s_gwp]:
        s.wait_send()


def reduce_call(gwo, dc_t, da_t, loss, g2, f2, w_enc, gf_shape, n_t):
    vm = pl.BlockSpec(memory_space=pltpu.VMEM)
    like = lambda x: pltpu.VMEM(x.shape, x.dtype)
    gwp_shape = (g2.shape[1], dc_t.shape[1])
    return pl.pallas_call(
        functools.partial(reduce_kernel, n_t),
        out_shape=(
            pltpu.VMEM((1, f2.shape[0] // n_t), F32),
            pltpu.VMEM(gf_shape, BF16),
            pltpu.VMEM(w_enc.shape, F32),
            pltpu.VMEM(gwp_shape, F32),
            pltpu.VMEM(gwo.shape, F32),
        ),
        in_specs=[vm] * 5 + [pl.BlockSpec(memory_space=pltpu.HBM)] * 2,
        out_specs=(vm,) * 5,
        scratch_shapes=[like(x) for x in (g2, w_enc)] + [
            pltpu.VMEM(gwp_shape, F32), like(gwo), pltpu.VMEM(gwp_shape, F32), like(da_t), like(loss), like(da_t),
            pltpu.SemaphoreType.DMA((2,)),
            pltpu.SemaphoreType.DMA((7,)),
            pltpu.SemaphoreType.DMA((7,)),
        ],
        compiler_params=pltpu.CompilerParams(collective_id=1, has_side_effects=True, vmem_limit_bytes=REDUCE_VMEM),
        name="rnnt_reduce",
    )(in_vmem(gwo), in_vmem(dc_t), in_vmem(da_t), in_vmem(loss), in_vmem(f2), in_hbm(g2), in_hbm(w_enc))


def store_kernel(n, *refs):
    sems = refs[2 * n]
    copies = [pltpu.make_async_copy(refs[q], refs[n + q], sems.at[q]) for q in range(n)]
    for copy in copies:
        copy.start()
    for copy in copies:
        copy.wait()


def store_call(arrays):
    n = len(arrays)
    return pl.pallas_call(
        functools.partial(store_kernel, n),
        out_shape=tuple(pltpu.HBM(x.shape, x.dtype) for x in arrays),
        in_specs=[pl.BlockSpec(memory_space=pltpu.VMEM)] * n,
        out_specs=(pl.BlockSpec(memory_space=pltpu.HBM),) * n,
        scratch_shapes=[pltpu.SemaphoreType.DMA((n,))],
        compiler_params=pltpu.CompilerParams(vmem_limit_bytes=STORE_VMEM),
        name="rnnt_store",
    )(*[in_vmem(x) for x in arrays])


def core_kernel(n_t, n_u, flen_s, llen_s, flen_v, llen_v, y_buf, c_buf, a_buf, wot, wo_h,
                loss_ref, segu, da_ref, gwo_ref,
                wo_ref, wo_sem, hbuf, hpar, ebuf, fac, mch, sch, vsb, ypar, ybuf, idx, dzb, dpb, zrow, sk, abuf, t1buf, t2buf,
                gocc, gocb, segt, tbl, off):
    n_utt = flen_s.shape[0]
    n_j = c_buf.shape[1]
    n_v = wo_ref.shape[1]
    gu = WIN * n_u
    gt = WIN * n_t
    n_diag = n_t + n_u - 1
    n_kt = (n_diag + 1) * n_t
    n_ch = n_v // CHUNK

    load_wo = pltpu.make_async_copy(wo_h, wo_ref, wo_sem)
    load_wo.start()

    total = jnp.int32(0)
    for b in range(n_utt):
        off[b] = total
        total = total + flen_s[b] * (llen_s[b] + 1)
    off[n_utt] = total

    cut = jnp.int32(CORE_MIN)
    for b in range(CORE_MIN, CORE_MAX):
        cut = cut + jnp.where(off[b] + off[b + 1] <= total, 1, 0)
    first_core = lax.axis_index('seq') % 2 == 0
    u_lo = jnp.where(first_core, 0, cut)
    u_hi = jnp.where(first_core, cut, n_utt)
    stop = off[u_hi]

    def utt_step(b, carry):
        win = jnp.minimum(b, n_utt - WIN)
        base = off[win]
        last = jnp.minimum(off[win + WIN], stop)

        def emit(c):
            n, pos = c
            end = jnp.minimum(pos + ROWS, last)
            tbl[0, n] = win
            tbl[1, n] = pos - base
            tbl[2, n] = end - base
            return n + 1, end
        return lax.while_loop(lambda c: c[1] < off[b + 1], emit, carry)
    n_blocks, _ = lax.fori_loop(u_lo, u_hi, utt_step, (jnp.int32(0), off[u_lo]))
    for past in range(3):
        for q in range(3):
            tbl[q, n_blocks + past] = 0

    sk[...] = jnp.zeros_like(sk)
    mch[...] = jnp.zeros_like(mch)
    sch[...] = jnp.ones_like(sch)
    zrow[...] = jnp.zeros_like(zrow)
    vsb[...] = jnp.zeros_like(vsb)
    dpb[...] = jnp.zeros_like(dpb)

    def onehot(n, index_row):
        return (lax.broadcasted_iota(jnp.int32, (n, ROWS), 0) == index_row)

    def as_bf16(mask):
        return jnp.where(mask, 1.0, 0.0).astype(BF16)

    def block_onehot(i):
        iota = lax.broadcasted_iota(jnp.int32, (gu + gt, ROWS), 0)
        return jnp.concatenate([as_bf16(iota[0:gu] == idx[i, 0:1]), as_bf16(iota[gu:] == idx[i, 1:2])], axis=0)

    sub8 = lax.broadcasted_iota(jnp.int32, (8, ROWS), 0)
    n_sub = CHUNK // 8

    def rows_of(win, width):
        return pl.ds(pl.multiple_of(win * width, width), WIN * width)

    def spread3(idx_b, parts):
        mask = lax.broadcasted_iota(jnp.int32, (CORE_MAX, ROWS), 0) == idx_b
        return jnp.concatenate([jnp.where(mask, part, 0.0) for part in parts]
                               + [jnp.zeros((128 - 3 * CORE_MAX, ROWS), F32)], axis=0).astype(BF16)

    def locate(i):
        win = tbl[0, i]
        r = tbl[1, i] + lax.broadcasted_iota(jnp.int32, (1, ROWS), 1)
        end_r = tbl[2, i]
        start = jnp.int32(0)
        bl = jnp.full((1, ROWS), -1, jnp.int32)
        w = jnp.zeros((1, ROWS), jnp.int32)
        u1 = jnp.ones((1, ROWS), jnp.int32)
        for j in range(WIN):
            u1_j = llen_s[win + j] + 1
            end = start + flen_s[win + j] * u1_j
            inside = (r >= start) & (r < jnp.minimum(end, end_r))
            bl = jnp.where(inside, j, bl)
            w = jnp.where(inside, r - start, w)
            u1 = jnp.where(inside, u1_j, u1)
            start = end
        valid = bl >= 0
        t = jnp.zeros((1, ROWS), jnp.int32)
        for j in range(1, n_t):
            t = t + jnp.where(w >= j * u1, 1, 0)
        u = w - t * u1
        idx_u = jnp.where(valid, bl * n_u + u, -1)
        idx_t = jnp.where(valid, gu + bl * n_t + t, -1)
        idx_kt = jnp.where(valid, (t + u) * n_t + t, -1)
        idx_b = jnp.where(valid, win + bl - u_lo, -1024)
        rows8 = lax.broadcasted_iota(jnp.int32, (8, ROWS), 0)
        idx[i] = jnp.where(rows8 == 0, idx_u, jnp.where(rows8 == 1, idx_t, jnp.where(rows8 == 2, idx_kt, idx_b)))

    half = n_j // 2

    def hidden(i, par):
        win = tbl[0, i]
        oh = jnp.concatenate([block_onehot(i), jnp.zeros((256 - gu - gt, ROWS), BF16)], axis=0)
        none = jnp.zeros((256 - gu - gt, n_j), BF16)
        cols = jnp.concatenate([c_buf[rows_of(win, n_u)], a_buf[rows_of(win, n_t)].astype(BF16), none], axis=0).T
        for q in range(2):
            rows = slice(q * half, (q + 1) * half)
            pre = dot(cols[rows], oh)
            h = jnp.tanh(pre).astype(BF16)
            hpar[par, rows] = h
            hbuf[i, rows] = h
        yy = dot(jnp.concatenate(
            [y_buf[rows_of(win, n_u)], jnp.zeros((256 - gu, 128), BF16)], axis=0).T[0:16], oh)
        y8 = jnp.broadcast_to((yy[0:1] * 32.0 + yy[1:2]).astype(jnp.int32), (8, ROWS))
        ypar[par] = y8
        ybuf[i] = y8

    def finish(i, par):
        idx_b = idx[i, 3:4]
        m_all = mch[par]
        m8 = jnp.max(m_all.reshape(n_ch, 8, ROWS), axis=0)
        m = jnp.max(m8, axis=0, keepdims=True)
        f_all = jnp.exp(m_all - m)
        s = jnp.sum(jnp.sum((sch[par] * f_all).reshape(n_ch, 8, ROWS), axis=0), axis=0, keepdims=True)
        fac[i] = f_all * (1.0 / s)
        lse = m + jnp.log(s)
        b_parts = split3(zrow[par, 8:9] - lse)
        l_parts = split3(jnp.sum(zrow[par, 0:8], axis=0, keepdims=True) - lse)
        vsb[par, 0:128] = spread3(idx_b, b_parts)
        vsb[par, 128:256] = spread3(idx_b, l_parts)

    def scatter(i, par, live):
        okt = as_bf16(onehot(n_kt, jnp.where(live, idx[i, 2:3], -1)))
        part = n_kt // 2
        for q in range(2):
            sk[q * part:(q + 1) * part] += dot(okt[q * part:(q + 1) * part], vsb[par], NT)

    def slot_of(i):
        return jnp.where(i < KEEP, i, KEEP + i % 2)

    def scores_part(i, par, chunks, lz):
        y8 = ypar[par]
        y_tile = lax.shift_right_logical(y8, 3)
        slot = slot_of(i)
        for c in chunks:
            z = dot(wot[c * CHUNK:(c + 1) * CHUNK, :], hpar[par])
            z3 = z.reshape(n_sub, 8, ROWS)
            for k in range(n_sub):
                lz = jnp.where(y_tile == c * n_sub + k, z3[k], lz)
            if c == 0:
                zrow[par, 8:16] = z[0:8, :]
            m_c = jnp.max(z3, axis=0)
            e3 = jnp.exp(z3 - m_c[None])
            ebuf[slot, c * CHUNK:(c + 1) * CHUNK, :] = e3.reshape(CHUNK, ROWS)
            mch[par, c * 8:(c + 1) * 8, :] = m_c
            sch[par, c * 8:(c + 1) * 8, :] = jnp.sum(e3, axis=0)
        if chunks[-1] == n_ch - 1:
            zrow[par, 0:8] = jnp.where(sub8 == jnp.bitwise_and(y8, 7), lz, 0.0)
        return lz

    def scores_of(i, par):
        scores_part(i, par, range(n_ch), jnp.zeros((8, ROWS), F32))

    def fwd_pair(p, carry):
        i = 2 * p
        finish(jnp.maximum(i - 1, 0), 1)
        hidden(i + 1, 1)
        scatter(jnp.maximum(i - 2, 0), 0, i > 1)
        scores_of(i, 0)
        hidden(i + 2, 0)
        scores_of(i + 1, 1)
        scatter(jnp.maximum(i - 1, 0), 1, i > 0)
        finish(i, 0)
        locate(i + 3)
        locate(i + 4)
        return carry

    def fwd_odd(p, carry):
        i = n_blocks - 1
        finish(jnp.maximum(i - 1, 0), 1)
        scatter(jnp.maximum(i - 2, 0), 0, i > 1)
        scores_of(i, 0)
        scatter(jnp.maximum(i - 1, 0), 1, i > 0)
        finish(i, 0)
        scatter(i, 0, True)
        return carry

    def fwd_even(p, carry):
        finish(n_blocks - 1, 1)
        scatter(n_blocks - 2, 0, True)
        scatter(n_blocks - 1, 1, True)
        return carry

    for first in range(3):
        locate(jnp.int32(first))
    hidden(jnp.int32(0), 0)
    lax.fori_loop(0, n_blocks // 2, fwd_pair, 0)
    lax.fori_loop(0, n_blocks % 2, fwd_odd, 0)
    lax.fori_loop(0, 1 - n_blocks % 2, fwd_even, 0)

    tt = lax.broadcasted_iota(jnp.int32, (n_t, 128), 0)
    def own_lanes(ref):
        x = jnp.concatenate([ref[...], jnp.zeros((1, 128 - n_utt), jnp.int32)], axis=1).astype(F32)
        return pltpu.roll(jnp.broadcast_to(x, (n_t, 128)), (128 - u_lo) % 128, 1).astype(jnp.int32)
    t_len = own_lanes(flen_v)
    u_len = own_lanes(llen_v)

    def scores(k):
        lo = k * n_t
        x, y = (v + pltpu.roll(v, 128 - CORE_MAX, 1) + pltpu.roll(v, 128 - 2 * CORE_MAX, 1)
                for v in (sk[lo:lo + n_t, 0:128], sk[lo:lo + n_t, 128:256]))
        uu = k - tt
        ok = (uu >= 0) & (tt < t_len)
        bl_k = jnp.where(ok & (uu <= u_len), x, NEG)
        lb_k = jnp.where(ok & (uu < u_len), y, NEG)
        return bl_k, lb_k

    alpha = jnp.where(tt == 0, 0.0, NEG).astype(F32)
    abuf[0] = alpha
    beta = jnp.full((n_t, 128), NEG, F32)
    sc = [scores(k) for k in range(n_diag)]
    for step in range(n_diag):
        if step > 0:
            bl_k, lb_k = sc[step - 1]
            p1 = jnp.where(tt == 0, NEG, pltpu.roll(alpha + bl_k, 1, 0))
            alpha = logadd(p1, alpha + lb_k)
            abuf[step] = alpha
        k = n_diag - 1 - step
        bl_k, lb_k = sc[k]
        up = jnp.where(tt == n_t - 1, jnp.where(u_len == k + 1 - n_t, 0.0, NEG), pltpu.roll(beta, n_t - 1, 0))
        t1 = up + bl_k
        t2 = beta + lb_k
        t1buf[k] = t1
        t2buf[k] = t2
        beta = jnp.where(tt >= t_len, jnp.where(k - tt == u_len, 0.0, NEG), logadd(t1, t2))
    segu[...] = jnp.zeros_like(segu)
    segt[...] = jnp.zeros_like(segt)
    log_p = beta[0:1, :]
    lane = lax.broadcasted_iota(jnp.int32, (n_t, 128), 1)
    loss_ref[...] = pltpu.roll(jnp.where(lane < u_hi - u_lo, -log_p, 0.0), u_lo, 1)
    lane_ok = lane < CORE_MAX
    for k in range(n_diag):
        for which, buf in enumerate((t1buf, t2buf)):
            occ = jnp.where(lane_ok, jnp.exp(jnp.minimum(abuf[k] + buf[k] - log_p, 0.0)), 0.0)
            hi, mid, lo = split3(occ)
            lo_row = which * n_kt + k * n_t
            gocc[lo_row:lo_row + n_t, :] = hi + pltpu.roll(mid, CORE_MAX, 1) + pltpu.roll(lo, 2 * CORE_MAX, 1)
    for which in range(2):
        gocc[which * n_kt + n_diag * n_t:(which + 1) * n_kt, :] = jnp.zeros((n_kt - n_diag * n_t, 128), F32)
    gocb[...] = gocc[...].astype(BF16)

    def again(first, count):
        def one(q, carry):
            i = first + q

            @pl.when(i >= KEEP)
            def _():
                def chunk(c, carry):
                    rows = pl.ds(pl.multiple_of(c * CHUNK, CHUNK), CHUNK)
                    z3 = dot(wot[rows, :], hbuf[i]).reshape(n_sub, 8, ROWS)
                    ebuf[KEEP + i % 2, rows, :] = jnp.exp(z3 - jnp.max(z3, axis=0)[None]).reshape(CHUNK, ROWS)
                    return carry
                lax.fori_loop(0, n_ch, chunk, 0)
            return carry
        @pl.when(first + count > KEEP)
        def _():
            lax.fori_loop(0, count, one, 0)

    def occupancy(i, par):
        orep = spread3(idx[i, 3:4], (1.0, 1.0, 1.0))
        kt8 = jnp.broadcast_to(idx[i, 2:3], (8, ROWS))
        kt_tile = lax.shift_right_arithmetic(kt8, 3)
        kt_sub = sub8 == jnp.bitwise_and(kt8, 7)
        for which in range(2):
            gath = dot(gocb[which * n_kt:(which + 1) * n_kt], orep).reshape(n_kt // 8, 8, ROWS)
            occ = jnp.zeros((8, ROWS), F32)
            for k in range(n_diag):
                occ = jnp.where(kt_tile == k, gath[k], occ)
            occ = jnp.sum(jnp.where(kt_sub, occ, 0.0), axis=0, keepdims=True)
            zrow[par, which * 8:which * 8 + 8] = jnp.broadcast_to(occ, (8, ROWS))

    def d_logits(i, par):
        y8 = ybuf[i]
        y_tile = lax.shift_right_logical(y8, 3)
        gb = zrow[par, 0:8]
        gl = zrow[par, 8:16]
        occ = gb + gl
        gl_y = jnp.where(sub8 == jnp.bitwise_and(y8, 7), gl, 0.0)
        gb_0 = jnp.where(sub8 == 0, gb, 0.0)
        slot = slot_of(i)
        for c in range(n_ch):
            sc_c = fac[i, c * 8:(c + 1) * 8, :] * occ
            e3 = ebuf[slot, c * CHUNK:(c + 1) * CHUNK, :].reshape(n_sub, 8, ROWS)
            tiles = []
            for k in range(n_sub):
                d = e3[k] * sc_c
                if c == 0 and k == 0:
                    d = d - gb_0
                tiles.append(d - jnp.where(y_tile == c * n_sub + k, gl_y, 0.0))
            d = jnp.concatenate(tiles, axis=0)
            dzb[par, c * CHUNK:(c + 1) * CHUNK, :] = d.astype(BF16)

    def segments(i, par):
        win = tbl[0, i]
        oh = block_onehot(i)
        for lo in range(0, n_j, 256):
            cols = slice(lo, min(lo + 256, n_j))
            sums = dot(oh, dpb[par, cols], NT)
            segu[rows_of(win, n_u), cols] += sums[0:gu]
            segt[rows_of(win, n_t), cols] += sums[gu:]

    def d_hidden(i, par):
        for q in range(2):
            rows = slice(q * half, (q + 1) * half)
            hf = hbuf[i, rows].astype(F32)
            dh = dot(wo_ref[rows], dzb[par])
            dpb[par, rows] = (dh * (1.0 - hf * hf)).astype(BF16)

    def out_grad(blocks, add):
        for c in range(n_v // 256):
            cols = slice(c * 256, (c + 1) * 256)
            new = None
            for i, par in blocks:
                term = dot(hbuf[i], dzb[par, cols, :], NT)
                new = term if new is None else new + term
            gwo_ref[:, cols] = jnp.where(add, gwo_ref[:, cols], 0.0) + new

    def bwd_pair(p, carry):
        i = 2 * p
        again(i + 2, 2)
        d_hidden(i, 0)
        d_hidden(i + 1, 1)
        segments(i, 0)
        segments(i + 1, 1)
        out_grad(((i, 0), (i + 1, 1)), p > 0)
        d_logits(i + 2, 0)
        d_logits(i + 3, 1)
        occupancy(i + 4, 0)
        occupancy(i + 5, 1)
        return carry

    def bwd_odd(p, carry):
        d_hidden(n_blocks - 1, 0)
        out_grad(((n_blocks - 1, 0),), n_blocks > 1)
        segments(n_blocks - 1, 0)
        return carry

    load_wo.wait()
    again(0, 2)
    for first in range(2):
        occupancy(jnp.int32(first), first)
        d_logits(jnp.int32(first), first)
        occupancy(jnp.int32(first + 2), first)
    lax.fori_loop(0, n_blocks // 2, bwd_pair, 0)
    lax.fori_loop(0, n_blocks % 2, bwd_odd, 0)

    da_ref[...] = segt[...].astype(BF16)


def core_call(c_t, a_t, wot, ylab, w_out, flen, llen, n_t, n_u):
    n_utt = flen.shape[0]
    n_j = c_t.shape[1]
    n_v = w_out.shape[1]
    max_blk = n_utt // 2 * n_t * n_u // ROWS + 6
    n_kt = (n_t + n_u) * n_t
    n_st = n_v // CHUNK * 8
    vm = pl.BlockSpec(memory_space=pltpu.VMEM)
    sm = pl.BlockSpec(memory_space=pltpu.SMEM)
    return pl.pallas_call(
        functools.partial(core_kernel, n_t, n_u),
        out_shape=(
            pltpu.VMEM((8, 128), F32),
            pltpu.VMEM((n_utt * n_u, n_j), F32),
            pltpu.VMEM((n_utt * n_t, n_j), BF16),
            pltpu.VMEM(w_out.shape, F32),
        ),
        in_specs=[sm, sm] + [vm] * 6 + [pl.BlockSpec(memory_space=pltpu.HBM)],
        out_specs=(vm,) * 4,
        scratch_shapes=[
            pltpu.VMEM(w_out.shape, BF16),
            pltpu.SemaphoreType.DMA,
            pltpu.VMEM((max_blk, n_j, ROWS), BF16),
            pltpu.VMEM((2, n_j, ROWS), BF16),
            pltpu.VMEM((min(max_blk, KEEP + 2), n_v, ROWS), F32),
            pltpu.VMEM((max_blk, n_st, ROWS), F32),
            pltpu.VMEM((2, n_st, ROWS), F32),
            pltpu.VMEM((2, n_st, ROWS), F32),
            pltpu.VMEM((2, 256, ROWS), BF16),
            pltpu.VMEM((2, 8, ROWS), jnp.int32),
            pltpu.VMEM((max_blk, 8, ROWS), jnp.int32),
            pltpu.VMEM((max_blk, 8, ROWS), jnp.int32),
            pltpu.VMEM((2, n_v, ROWS), BF16),
            pltpu.VMEM((2, n_j, ROWS), BF16),
            pltpu.VMEM((2, 16, ROWS), F32),
            pltpu.VMEM((n_kt, 256), F32),
            pltpu.VMEM((n_t + n_u, n_t, 128), F32),
            pltpu.VMEM((n_t + n_u, n_t, 128), F32),
            pltpu.VMEM((n_t + n_u, n_t, 128), F32),
            pltpu.VMEM((2 * n_kt, 128), F32),
            pltpu.VMEM((2 * n_kt, 128), BF16),
            pltpu.VMEM((n_utt * n_t, n_j), F32),
            pltpu.SMEM((3, max_blk), jnp.int32),
            pltpu.SMEM((n_utt + 1,), jnp.int32),
        ],
        compiler_params=pltpu.CompilerParams(vmem_limit_bytes=CORE_VMEM),
        name="rnnt_core",
    )(flen, llen, flen.reshape(1, n_utt), llen.reshape(1, n_utt), *[in_vmem(x) for x in (ylab, c_t, a_t, wot)], in_hbm(w_out))


def solution(mesh):
    seq_size = mesh.shape['seq']

    def local_fn(enc_out, pred_out, w_enc, w_pred, w_out, labels, frame_len, label_len):
        n_utt, n_loc, n_h = enc_out.shape
        n_u = pred_out.shape[1]
        n_t = n_loc * seq_size
        g2 = pred_out.reshape(n_utt * n_u, n_h)
        c_t, a_t, wot, f2, *rest = gather_call(enc_out, g2, w_enc, w_pred, w_out, labels.T, seq_size, n_t, n_u)
        loss, dc_t, da_t, gwo = core_call(c_t, a_t, wot, *rest, w_out, frame_len, label_len, n_t, n_u)
        loss, gf, gwe, gwp, gwo = store_call(reduce_call(gwo, dc_t, da_t, loss, g2, f2, w_enc, enc_out.shape, n_t))
        return loss.reshape(n_utt), gf, gwe, gwp, gwo

    in_specs = (P('dp', 'seq', None), P('dp', None, None), P(None, None), P(None, None), P(None, None), P('dp', None), P('dp'), P('dp'))
    out_specs = (P('dp'), P('dp', 'seq', None), P('dp', None), P('dp', None), P('dp', None))
    return jax.shard_map(local_fn, mesh=mesh, in_specs=in_specs, out_specs=out_specs, check_vma=False)
```

profile of v0, /device:TPU:0, one launch (start us, length us, event | category | flops | bytes accessed | tf_op | source)
XLA Modules:
  0.0 50.6 jit_solution(1114748780189119497)
XLA Ops:
  0.6 9.6 %rnnt_gather.1 = (bf16[2048,640]{1,0:T(8,128)(2,1)S(1)}, f32[512,640]{1,0:T(8,128)S(1)}, bf16[1024,640]{1,0:T(8,128)(2,1)S(1)}, bf16[512,640]{1,0:T(8,128)(2,1)S(1)}, bf16[2048,128]{1,0:T(8,128)(2,1)S(1)}) custom-call(bf16[64,2,640]{2,1,0:T(2,128)(2,1)} %enc_h.1, bf16[2048,640]{1,0:T(8,128)(2,1)} %bitcast.5, bf16[640,640]{1,0:T(8,128)(2,1)} %we_p.1, ...), custom_call_target="tpu_custom_call" | custom-call | tf_op jit(solution)/shard_map/rnnt_gather/pallas_call | solution.py:134
  10.2 28.1 %rnnt_core.1 = (f32[8,128]{1,0:T(8,128)S(1)}, f32[2048,640]{1,0:T(8,128)S(1)}, bf16[512,640]{1,0:T(8,128)(2,1)S(1)}, f32[640,1024]{1,0:T(8,128)S(1)}) custom-call(s32[64]{0:T(128)} %flen_s.1, s32[64]{0:T(128)} %llen_s.1, s32[1,64]{1,0:T(1,128)} %bitcast.8, s32[1,64]{1,0:T(1,128)} %bitcast.9, bf16[2048,128]{1,0:T(8,128)(2,1)S(1)} %get-tuple-element.24.y_buf, ...), custom_call_target="tpu_custom_call" | custom-call | tf_op jit(solution)/shard_map/rnnt_core/pallas_call | solution.py:633
  38.3 9.5 %rnnt_reduce.1 = (f32[1,64]{1,0:T(1,128)S(1)}, bf16[64,2,640]{2,1,0:T(2,128)(2,1)S(1)}, f32[640,640]{1,0:T(8,128)S(1)}, f32[640,640]{1,0:T(8,128)S(1)}, f32[640,1024]{1,0:T(8,128)S(1)}) custom-call(f32[640,1024]{1,0:T(8,128)S(1)} %get-tuple-element.28.gwo_v, f32[2048,640]{1,0:T(8,128)S(1)} %get-tuple-element.29.dc_v, ...), custom_call_target="tpu_custom_call" | custom-call | tf_op jit(solution)/shard_map/rnnt_reduce/pallas_call | solution.py:215
  47.8 2.7 %rnnt_store.1 = (f32[1,64]{1,0:T(1,128)}, bf16[64,2,640]{2,1,0:T(2,128)(2,1)}, f32[640,640]{1,0:T(8,128)}, f32[640,640]{1,0:T(8,128)}, f32[640,1024]{1,0:T(8,128)}) custom-call(f32[1,64]{1,0:T(1,128)S(1)} %get-tuple-element.33.refs_0_, bf16[64,2,640]{2,1,0:T(2,128)(2,1)S(1)} %get-tuple-element.34.refs_1_, f32[640,640]{1,0:T(8,128)S(1)} %get-tuple-element.35.refs_2_, ...), custom_call_target="tpu_custom_call" | custom-call | tf_op jit(solution)/shard_map/rnnt_store/pallas_call | solution.py:248
where the time goes:
time: 51.4 us; the launch traced here: 50.6 us
  Pallas kernels  49.8 us (97%)
  between operations  0.82 us (2%)
    pallas_call x1, Pallas kernels, core_call(): pl.pallas_call(functools.partial(core_kernel, n_t, n_u), out_shape=(pltpu...  28.1 us
    pallas_call x1, Pallas kernels, gather_call(): pl.pallas_call(functools.partial(gather_kernel, n_t, n_u), out_shape=(plt...  9.56 us
    pallas_call x1, Pallas kernels, reduce_call(): pl.pallas_call(functools.partial(reduce_kernel, n_t), out_shape=(pltpu.VM...  9.46 us
    pallas_call x1, Pallas kernels, store_call(): pl.pallas_call(functools.partial(store_kernel, n), out_shape=tuple((pltpu...  2.68 us

commit v1 on v0

--- a/solution.py
+++ b/solution.py
@@ -74,27 +74,39 @@
         ((enc_h, enc_ref), (wo_h, wo_ref), (wp_h, wp_ref), (g_h, g_ref), (we_h, we_ref), (lab_h, lab_ref)))]
     for load in loads:
         load.start()
+    diag = (partner + 2) % n_seq
     barrier = pltpu.get_barrier_semaphore()
-    for other in (partner, peer):
+    for other in (partner, peer, diag):
         pl.semaphore_signal(barrier, inc=1, device_id={'seq': other}, device_id_type=MESH)
-    pl.semaphore_wait(barrier, 2)
-
-    def send(src, slot, sem, other):
-        return pltpu.make_async_remote_copy(src_ref=src, dst_ref=fbuf.at[slot], send_sem=send_sem.at[sem], recv_sem=recv_sem.at[sem],
-                                            device_id={'seq': other}, device_id_type=MESH)
+    pl.semaphore_wait(barrier, 3)
+
+    core = me % 2
+    n_utt = enc_ref.shape[0]
+    n_need = CORE_MAX + 8
+    n_edge = n_utt - n_need
+    middle = pl.ds(n_edge, n_utt - 2 * n_edge)
+    edge = lambda c: pl.ds(c * n_need, n_edge)
+
+    def send(src, slot, part, sem, other):
+        return pltpu.make_async_remote_copy(src_ref=src.at[part], dst_ref=fbuf.at[slot, part], send_sem=send_sem.at[sem],
+                                            recv_sem=recv_sem.at[sem], device_id={'seq': other}, device_id_type=MESH)
     load_enc.wait()
-    to_peer = send(enc_ref, me, 0, peer)
-    to_peer.start()
-    to_partner = send(enc_ref, me, 1, partner)
-    to_partner.start()
+    sends = [
+        send(enc_ref, me, middle, 0, peer),
+        send(enc_ref, me, edge(core), 1, peer),
+        send(enc_ref, me, edge(1 - core), 2, diag),
+        send(enc_ref, me, pl.ds((1 - core) * n_edge, n_need), 3, partner),
+    ]
+    for s in sends:
+        s.start()
+    fbuf[:, edge(1 - core)] = jnp.zeros((n_seq, n_edge) + fbuf.shape[2:], BF16)
     fbuf[me] = enc_ref[...]
     load_wo.wait()
     wot_ref[...] = wo_ref[...].T
     load_wp.wait()
     load_g.wait()
-    n_own_utt = CORE_MAX + WIN
-    n_c = n_own_utt * n_u
-    first = me % 2 * (c_ref.shape[0] // n_u - n_own_utt)
+    n_c = n_need * n_u
+    first = core * n_edge
     rows_c = pl.ds(pl.multiple_of(first * n_u, 64), n_c)
     c_ref[rows_c, :] = dot(g_ref[rows_c, :], wp_ref[...]).astype(BF16)
     load_we.wait()
@@ -112,17 +124,18 @@
         order = jnp.where(col == row // n_loc * n_t + p * n_loc + row % n_loc, 1.0, 0.0).astype(BF16)
         return dot(order, dot(rows, we_ref[...]).astype(BF16))
     a_t = piece(me)
-    to_partner.wait_recv()
+    sends[3].wait_recv()
     a_t = a_t + piece(partner)
-    to_peer.wait_recv()
-    relay = send(fbuf.at[peer], peer, 2, partner)
+    sends[0].wait_recv()
+    relay = send(fbuf.at[peer], peer, middle, 4, partner)
     relay.start()
+    sends[1].wait_recv()
     a_t = a_t + piece(peer)
+    sends[2].wait_recv()
     relay.wait_recv()
-    a_ref[...] = a_t + piece((partner + 2) % n_seq)
-    to_peer.wait_send()
-    to_partner.wait_send()
-    relay.wait_send()
+    a_ref[...] = a_t + piece(diag)
+    for s in sends + [relay]:
+        s.wait_send()
 
 
 def gather_call(enc, g2, w_enc, w_pred, w_out, labels_t, n_seq, n_t, n_u):
@@ -145,8 +158,8 @@
         scratch_shapes=[pltpu.VMEM(x.shape, x.dtype) for x in (enc, g2, w_enc, w_pred, w_out, labels_t)] + [
             pltpu.VMEM((n_seq, n_utt, n_loc, n_h), BF16),
             pltpu.SemaphoreType.DMA((6,)),
-            pltpu.SemaphoreType.DMA((3,)),
-            pltpu.SemaphoreType.DMA((3,)),
+            pltpu.SemaphoreType.DMA((5,)),
+            pltpu.SemaphoreType.DMA((5,)),
         ],
         compiler_params=pltpu.CompilerParams(collective_id=0, has_side_effects=True, vmem_limit_bytes=GATHER_VMEM),
         name="rnnt_gather",
@@ -154,7 +167,7 @@
 
 
 def reduce_kernel(n_t, gwo_v, dc_v, da_v, loss_v, f_v, g_p, we_p, loss_ref, gf_ref, gwe_ref, gwp_ref, gwo_ref,
-                  g_v, we_v, gwp_v, rgwo, rgwp, rda, rloss, da_rows, in_sem, send_sem, recv_sem):
+                  g_v, we_v, gwp_v, rgwo, rgwp, rda, rloss, da_rows, rf, f_all, in_sem, send_sem, recv_sem):
     me = lax.axis_index('seq')
     partner = me + 1 - 2 * (me % 2)
     loads = [pltpu.make_async_copy(src, dst, in_sem.at[q]) for q, (src, dst) in enumerate(((g_p, g_v), (we_p, we_v)))]
@@ -174,7 +187,12 @@
     part = pl.ds(pl.multiple_of(da_lo, 64), n_da)
     sends = [send(da_v.at[part], rda.at[part], 0), send(loss_v, rloss, 1)]
     sends += [send(gwo_v.at[pl.ds(q * rows, rows)], rgwo.at[pl.ds(q * rows, rows)], 2 + q) for q in range(n_part)]
-    for s in sends:
+    n_dev = n_t // gf_ref.shape[1]
+    n_blk = f_v.shape[0] // n_dev
+    n_edge = rf.shape[0] // n_dev
+    edge_lo = lambda p, c: pl.multiple_of(p * n_blk + c * (n_blk - n_edge), 16)
+    f_sends = [send(f_v.at[pl.ds(edge_lo(p, me % 2), n_edge)], rf.at[pl.ds(p * n_edge, n_edge)], 3 + n_part + p) for p in range(n_dev)]
+    for s in sends + f_sends:
         s.start()
     loads[0].wait()
     gwp_v[...] = dot(g_v[...].T, dc_v[...].astype(BF16))
@@ -195,7 +213,11 @@
     order = jnp.where(col == row % n_own // n_loc * n_t + row // n_own * n_loc + row % n_loc, 1.0, 0.0).astype(BF16)
     da_f = dot(order, da).astype(BF16)
     da_rows[...] = da_f
-    gwe_ref[...] = dot(f_v[...].T, da_f)
+    f_all[...] = f_v[...]
+    for p in range(n_dev):
+        f_sends[p].wait_recv()
+        f_all[pl.ds(edge_lo(p, partner % 2), n_edge), :] = rf[p * n_edge:(p + 1) * n_edge]
+    gwe_ref[...] = dot(f_all[...].T, da_f)
     own = da_rows[pl.ds(pl.multiple_of(me * n_own, n_own), n_own), :]
     gf_ref[...] = dot(own, we_v[...], NT).astype(BF16).reshape(gf_ref.shape)
     for q in range(n_part):
@@ -204,7 +226,7 @@
         gwo_ref[part] = gwo_v[part] + rgwo[part]
     s_gwp.wait_recv()
     gwp_ref[...] = gwp_v[...] + rgwp[...]
-    for s in sends + [s_gwp]:
+    for s in sends + f_sends + [s_gwp]:
         s.wait_send()
 
 
@@ -224,10 +246,10 @@
         in_specs=[vm] * 5 + [pl.BlockSpec(memory_space=pltpu.HBM)] * 2,
         out_specs=(vm,) * 5,
         scratch_shapes=[like(x) for x in (g2, w_enc)] + [
-            pltpu.VMEM(gwp_shape, F32), like(gwo), pltpu.VMEM(gwp_shape, F32), like(da_t), like(loss), like(da_t),
+            pltpu.VMEM(gwp_shape, F32), like(gwo), pltpu.VMEM(gwp_shape, F32), like(da_t), like(loss), like(da_t), pltpu.VMEM(((gf_shape[0] - CORE_MAX - 8) * n_t, f2.shape[1]), BF16), like(f2),
             pltpu.SemaphoreType.DMA((2,)),
-            pltpu.SemaphoreType.DMA((7,)),
-            pltpu.SemaphoreType.DMA((7,)),
+            pltpu.SemaphoreType.DMA((11,)),
+            pltpu.SemaphoreType.DMA((11,)),
         ],
         compiler_params=pltpu.CompilerParams(collective_id=1, has_side_effects=True, vmem_limit_bytes=REDUCE_VMEM),
         name="rnnt_reduce",

time: 51.4 us -> 51.3 us (level)
  the two profiles are of different devices: /device:TPU:0 before, /device:TPU:9 now
where the time goes in v1:
time: 51.3 us; the launch traced here: 51.7 us
  Pallas kernels  50.9 us (99%)
  between operations  0.82 us (2%)
    pallas_call x1, Pallas kernels, core_call(): pl.pallas_call(functools.partial(core_kernel, n_t, n_u), out_shape=(pltpu...  31.3 us
    pallas_call x1, Pallas kernels, reduce_call(): pl.pallas_call(functools.partial(reduce_kernel, n_t), out_shape=(pltpu.VM...  8.5 us
    pallas_call x1, Pallas kernels, gather_call(): pl.pallas_call(functools.partial(gather_kernel, n_t, n_u), out_shape=(plt...  8.47 us
    pallas_call x1, Pallas kernels, store_call(): pl.pallas_call(functools.partial(store_kernel, n), out_shape=tuple((pltpu...  2.68 us

profile of v1, /device:TPU:9, one launch (start us, length us, event | category | flops | bytes accessed | tf_op | source)
XLA Modules:
  0.0 51.7 jit_solution(11851704462296587790)
XLA Ops:
  0.6 8.5 %rnnt_gather.1 = (bf16[2048,640]{1,0:T(8,128)(2,1)S(1)}, f32[512,640]{1,0:T(8,128)S(1)}, bf16[1024,640]{1,0:T(8,128)(2,1)S(1)}, bf16[512,640]{1,0:T(8,128)(2,1)S(1)}, bf16[2048,128]{1,0:T(8,128)(2,1)S(1)}) custom-call(bf16[64,2,640]{2,1,0:T(2,128)(2,1)} %enc_h.1, bf16[2048,640]{1,0:T(8,128)(2,1)} %bitcast.5, bf16[640,640]{1,0:T(8,128)(2,1)} %we_p.1, ...), custom_call_target="tpu_custom_call" | custom-call | tf_op jit(solution)/shard_map/rnnt_gather/pallas_call | solution.py:147
  9.1 31.3 %rnnt_core.1 = (f32[8,128]{1,0:T(8,128)S(1)}, f32[2048,640]{1,0:T(8,128)S(1)}, bf16[512,640]{1,0:T(8,128)(2,1)S(1)}, f32[640,1024]{1,0:T(8,128)S(1)}) custom-call(s32[64]{0:T(128)} %flen_s.1, s32[64]{0:T(128)} %llen_s.1, s32[1,64]{1,0:T(1,128)} %bitcast.8, s32[1,64]{1,0:T(1,128)} %bitcast.9, bf16[2048,128]{1,0:T(8,128)(2,1)S(1)} %get-tuple-element.24.y_buf, ...), custom_call_target="tpu_custom_call" | custom-call | tf_op jit(solution)/shard_map/rnnt_core/pallas_call | solution.py:655
  40.4 8.5 %rnnt_reduce.1 = (f32[1,64]{1,0:T(1,128)S(1)}, bf16[64,2,640]{2,1,0:T(2,128)(2,1)S(1)}, f32[640,640]{1,0:T(8,128)S(1)}, f32[640,640]{1,0:T(8,128)S(1)}, f32[640,1024]{1,0:T(8,128)S(1)}) custom-call(f32[640,1024]{1,0:T(8,128)S(1)} %get-tuple-element.28.gwo_v, f32[2048,640]{1,0:T(8,128)S(1)} %get-tuple-element.29.dc_v, ...), custom_call_target="tpu_custom_call" | custom-call | tf_op jit(solution)/shard_map/rnnt_reduce/pallas_call | solution.py:237
  48.9 2.7 %rnnt_store.1 = (f32[1,64]{1,0:T(1,128)}, bf16[64,2,640]{2,1,0:T(2,128)(2,1)}, f32[640,640]{1,0:T(8,128)}, f32[640,640]{1,0:T(8,128)}, f32[640,1024]{1,0:T(8,128)}) custom-call(f32[1,64]{1,0:T(1,128)S(1)} %get-tuple-element.33.refs_0_, bf16[64,2,640]{2,1,0:T(2,128)(2,1)S(1)} %get-tuple-element.34.refs_1_, f32[640,640]{1,0:T(8,128)S(1)} %get-tuple-element.35.refs_2_, ...), custom_call_target="tpu_custom_call" | custom-call | tf_op jit(solution)/shard_map/rnnt_store/pallas_call | solution.py:270
